TPU v7x, 8 devices: a whole 2x2x1 slice. The times are simulated.
8 devices in a mesh: rep: 1 (over z), dp: 8 (over x, y, core).
Axes of the slice: x: 2, y: 2, z: 1, core: 2. Of those that a mesh axis runs over, the one named last changes fastest.
Arguments:
- g_w_gate: bfloat16 [8, 2, 512, 8192], P(('rep', 'dp'))
- g_w_up: bfloat16 [8, 2, 512, 8192], P(('rep', 'dp'))
- g_w_down: bfloat16 [8, 2, 8192, 512], P(('rep', 'dp'))
- w_gate: bfloat16 [2, 512, 8192], replicated
- w_up: bfloat16 [2, 512, 8192], replicated
- w_down: bfloat16 [2, 8192, 512], replicated
- m_w_gate: float32 [2, 512, 8192], P(None, 'dp')
- m_w_up: float32 [2, 512, 8192], P(None, 'dp')
- m_w_down: float32 [2, 8192, 512], P(None, 'dp')
- v_w_gate: float32 [2, 512, 8192], P(None, 'dp')
- v_w_up: float32 [2, 512, 8192], P(None, 'dp')
- v_w_down: float32 [2, 8192, 512], P(None, 'dp')
Outputs:
- output 1: bfloat16 [2, 512, 8192], P('rep')
- output 2: bfloat16 [2, 512, 8192], P('rep')
- output 3: bfloat16 [2, 8192, 512], P('rep')
- output 4: float32 [2, 512, 8192], P('rep', 'dp')
- output 5: float32 [2, 512, 8192], P('rep', 'dp')
- output 6: float32 [2, 8192, 512], P('rep', 'dp')
- output 7: float32 [2, 512, 8192], P('rep', 'dp')
- output 8: float32 [2, 512, 8192], P('rep', 'dp')
- output 9: float32 [2, 8192, 512], P('rep', 'dp')
All inputs are finite; a program needn't handle non-finite values.
Results may differ from a plain program's by a relative error of at most 0.022.
Values are sent between devices in bfloat16 or wider.
A program may use at most 2 GiB of HBM per device.

v0:
```python
import jax
import jax.numpy as jnp
from jax import lax
from jax.sharding import PartitionSpec as P


def adamw(w, m, v, g):
    m = 0.9 * m + 0.1 * g
    v = 0.95 * v + 0.05 * g * g
    step = m * lax.rsqrt(v + 1e-8) + 0.1 * w
    return (w - 0.02 * step).astype(jnp.bfloat16), m, v


def solution(mesh):
    def step(*arrays):
        terms, weights, m, v = (arrays[i : i + 3] for i in (0, 3, 6, 9))
        gradients = [lax.psum_scatter(t[0], "dp", scatter_dimension=1, tiled=True).astype(jnp.float32) for t in terms]
        me = lax.axis_index("dp")
        own = [lax.dynamic_slice_in_dim(w, me * one.shape[1], one.shape[1], 1).astype(jnp.float32) for w, one in zip(weights, m, strict=True)]
        new = [adamw(w, m, v, g) for w, m, v, g in zip(own, m, v, gradients, strict=True)]
        whole = [lax.all_gather(one[0], "dp", axis=1, tiled=True) for one in new]
        return (*whole, *(one[1] for one in new), *(one[2] for one in new))

    all_of, cut = P(None, None, None), P(None, "dp", None)
    return jax.shard_map(
        step,
        mesh=mesh,
        in_specs=(P(("rep", "dp"), None, None, None),) * 3 + (all_of,) * 3 + (cut,) * 6,
        out_specs=(P("rep", None, None),) * 3 + (P("rep", "dp", None),) * 6,
        check_vma=False,
    )
```

profile of v0, /device:TPU:0, one launch (start us, length us, event | category | flops | bytes accessed | tf_op | source)
XLA Modules:
  0.0 642.2 jit_solution(13566426705269844911)
XLA Ops:
  7.2 0.0 reduce-scatter.8.cloned.1.call-start
  7.2 0.7 reduce-scatter.8.cloned.1.call-update
  7.9 0.0 reduce-scatter.6.cloned.1.call-start
  8.0 0.7 reduce-scatter.6.cloned.1.call-update
  8.7 0.0 reduce-scatter.4.cloned.1.call-start
  8.7 0.7 reduce-scatter.4.cloned.1.call-update
  9.4 0.0 all-gather.8.cloned.1.call-start
  9.4 111.8 %reduce-scatter.8.cloned.1.call-done = bf16[2,1024,512]{2,1,0:T(8,128)(2,1)} async-done(((bf16[2,8192,512]{2,1,0:T(8,128)(2,1)}), bf16[2,1024,512]{2,1,0:T(8,128)(2,1)}) %reduce-scatter.8.cloned.1.call-update) | async-done | bytes 2097168 | tf_op jit(solution)/shard_map/reduce_scatter | solution.py:17
  121.3 8.3 %fusion.10 = (bf16[2,1024,512]{2,1,0:T(8,128)(2,1)}, f32[2,1024,512]{2,1,0:T(8,128)}, f32[2,1024,512]{2,1,0:T(8,128)}) fusion(bf16[2,8192,512]{2,1,0:T(8,128)(2,1)} %param.17, s32[]{:T(128)S(6)} %select_n.8, bf16[2,1024,512]{2,1,0:T(8,128)(2,1)} %reduce-scatter.8.cloned.1.call-done, f32[2,1024,512]{2,1,0:T(8,128)} %param.23, f32[2,1024,512]{2,1,0:T(8,128)} %param.20), kind=kLoop, calls=%fused_computation.22 | loop fusion | flops 16777216 | bytes 23068676 | tf_op jit(solution)/shard_map/convert_element_type | solution.py:11
  129.6 0.0 all-gather.8.cloned.1.call-update
  129.6 0.0 all-gather.6.cloned.1.call-start
  129.7 102.1 %reduce-scatter.6.cloned.1.call-done = bf16[2,64,8192]{2,1,0:T(8,128)(2,1)} async-done(((bf16[2,512,8192]{2,1,0:T(8,128)(2,1)}), bf16[2,64,8192]{2,1,0:T(8,128)(2,1)}) %reduce-scatter.6.cloned.1.call-update) | async-done | bytes 2097168 | tf_op jit(solution)/shard_map/reduce_scatter | solution.py:17
  231.8 8.4 %fusion.6 = (bf16[2,64,8192]{2,1,0:T(8,128)(2,1)}, f32[2,64,8192]{2,1,0:T(8,128)}, f32[2,64,8192]{2,1,0:T(8,128)}) fusion(bf16[2,512,8192]{2,1,0:T(8,128)(2,1)} %param.16, s32[]{:T(128)S(6)} %select_n.7, bf16[2,64,8192]{2,1,0:T(8,128)(2,1)} %reduce-scatter.6.cloned.1.call-done, f32[2,64,8192]{2,1,0:T(8,128)} %param.22, f32[2,64,8192]{2,1,0:T(8,128)} %param.19), kind=kLoop, calls=%fused_computation.18 | loop fusion | flops 16777216 | bytes 23068676 | tf_op jit(solution)/shard_map/convert_element_type | solution.py:11
  240.2 0.0 all-gather.4.cloned.1.call-start
  240.2 102.0 %reduce-scatter.4.cloned.1.call-done = bf16[2,64,8192]{2,1,0:T(8,128)(2,1)} async-done(((bf16[2,512,8192]{2,1,0:T(8,128)(2,1)}), bf16[2,64,8192]{2,1,0:T(8,128)(2,1)}) %reduce-scatter.4.cloned.1.call-update) | async-done | bytes 2097168 | tf_op jit(solution)/shard_map/reduce_scatter | solution.py:17
  342.2 8.4 %fusion.2 = (bf16[2,64,8192]{2,1,0:T(8,128)(2,1)}, f32[2,64,8192]{2,1,0:T(8,128)}, f32[2,64,8192]{2,1,0:T(8,128)}) fusion(bf16[2,512,8192]{2,1,0:T(8,128)(2,1)} %param.15, s32[]{:T(128)S(6)} %select_n.7, bf16[2,64,8192]{2,1,0:T(8,128)(2,1)} %reduce-scatter.4.cloned.1.call-done, f32[2,64,8192]{2,1,0:T(8,128)} %param.21, f32[2,64,8192]{2,1,0:T(8,128)} %param.18), kind=kLoop, calls=%fused_computation.14 | loop fusion | flops 16777216 | bytes 23068676 | tf_op jit(solution)/shard_map/convert_element_type | solution.py:11
  350.7 77.9 %all-gather.8.cloned.1.call-done = bf16[2,8192,512]{2,1,0:T(8,128)(2,1)} async-done(((bf16[2,1024,512]{2,1,0:T(8,128)(2,1)}), bf16[2,8192,512]{2,1,0:T(8,128)(2,1)}) %all-gather.8.cloned.1.call-update) | async-done | bytes 16777232 | tf_op jit(solution)/shard_map/all_gather | solution.py:21
  428.6 86.4 %all-gather.6.cloned.1.call-done = bf16[2,512,8192]{2,1,0:T(8,128)(2,1)} async-done(((bf16[2,64,8192]{2,1,0:T(8,128)(2,1)}), bf16[2,512,8192]{2,1,0:T(8,128)(2,1)}) %all-gather.6.cloned.1.call-update) | async-done | bytes 16777232 | tf_op jit(solution)/shard_map/all_gather | solution.py:21
  515.0 86.4 %all-gather.4.cloned.1.call-done = bf16[2,512,8192]{2,1,0:T(8,128)(2,1)} async-done(((bf16[2,64,8192]{2,1,0:T(8,128)(2,1)}), bf16[2,512,8192]{2,1,0:T(8,128)(2,1)}) %all-gather.4.cloned.1.call-update) | async-done | bytes 16777232 | tf_op jit(solution)/shard_map/all_gather | solution.py:21
  601.3 16.7 %copy.24 = bf16[2,512,8192]{2,1,0:T(8,128)(2,1)} copy(bf16[2,512,8192]{2,1,0:T(8,128)(2,1)} %all-gather.4.cloned.1.call-done) | data formatting | bytes 33554432
  618.0 8.5 %copy.25 = bf16[2,512,8192]{2,1,0:T(8,128)(2,1)} copy(bf16[2,512,8192]{2,1,0:T(8,128)(2,1)S(1)} %copy-done) | data formatting | bytes 33554432
  626.5 1.5 slice-done.2
  628.0 1.2 slice-done.3
  629.2 6.2 copy.26
  (11 shorter events, 0.0 us)
Async XLA Ops:
  7.2 114.1 %reduce-scatter.8.cloned.1.call-start = ((), (), s32[]{:S(2)}) async-start(), calls=%async_computation.7 | async-start | bytes 18874368 | tf_op jit(solution)/shard_map/reduce_scatter | solution.py:17
  7.9 223.8 %reduce-scatter.6.cloned.1.call-start = ((), (), s32[]{:S(2)}) async-start(), calls=%async_computation.5 | async-start | bytes 18874368 | tf_op jit(solution)/shard_map/reduce_scatter | solution.py:17
  8.7 333.6 %reduce-scatter.4.cloned.1.call-start = ((), (), s32[]{:S(2)}) async-start(), calls=%async_computation.3 | async-start | bytes 18874368 | tf_op jit(solution)/shard_map/reduce_scatter | solution.py:17
  9.4 419.2 %all-gather.8.cloned.1.call-start = ((), (), s32[]{:S(2)}) async-start(), calls=%async_computation.8 | async-start | bytes 18874368 | tf_op jit(solution)/shard_map/all_gather | solution.py:21
  129.6 385.4 %all-gather.6.cloned.1.call-start = ((), (), s32[]{:S(2)}) async-start(), calls=%async_computation.6 | async-start | bytes 18874368 | tf_op jit(solution)/shard_map/all_gather | solution.py:21
  240.2 361.2 %all-gather.4.cloned.1.call-start = ((), (), s32[]{:S(2)}) async-start(), calls=%async_computation.4 | async-start | bytes 18874368 | tf_op jit(solution)/shard_map/all_gather | solution.py:21
  601.3 16.7 %copy-start = (bf16[2,512,8192]{2,1,0:T(8,128)(2,1)S(1)}, bf16[2,512,8192]{2,1,0:T(8,128)(2,1)}, u32[]{:S(2)}) copy-start(bf16[2,512,8192]{2,1,0:T(8,128)(2,1)} %all-gather.6.cloned.1.call-done) | copy-start | bytes 50331652
  601.3 25.2 %slice-start = ((s8[16777216]{0:T(1024)(128)(4,1)}), s8[4194304]{0:T(1024)(128)(4,1)S(1)}, s32[]{:S(2)}) async-start(s8[16777216]{0:T(1024)(128)(4,1)} %bitcast.6), calls=%async_computation.9 | async-start | bytes 8388608
  601.3 25.2 %slice-start.1 = ((s8[16777216]{0:T(1024)(128)(4,1)}), s8[4194304]{0:T(1024)(128)(4,1)S(1)}, s32[]{:S(2)}) async-start(s8[16777216]{0:T(1024)(128)(4,1)} %bitcast.6), calls=%async_computation.10 | async-start | bytes 8388608
  618.0 10.0 %slice-start.2 = ((s8[16777216]{0:T(1024)(128)(4,1)}), s8[4194304]{0:T(1024)(128)(4,1)S(1)}, s32[]{:S(2)}) async-start(s8[16777216]{0:T(1024)(128)(4,1)} %bitcast.6), calls=%async_computation.11 | async-start | bytes 8388608
  618.0 11.2 %slice-start.3 = ((s8[16777216]{0:T(1024)(128)(4,1)}), s8[4194304]{0:T(1024)(128)(4,1)S(1)}, s32[]{:S(2)}) async-start(s8[16777216]{0:T(1024)(128)(4,1)} %bitcast.6), calls=%async_computation.12 | async-start | bytes 8388608
Sparse Core Ops, SparseCore 0:
  11.5 109.7 reduce-scatter.7
  124.8 106.9 reduce-scatter.5
  235.3 106.9 reduce-scatter.3
  344.5 84.0 all-gather.7
  430.9 84.0 all-gather.5
  517.2 84.0 all-gather.3
where the time goes:
time: 642 us
  waiting for transfers between devices  569 us (89%)
  local copies, waits for them, and re-layouts  34.1 us (5%)
  other arithmetic  25.1 us (4%)
  between operations  14.1 us (2%)
    reduce_scatter x3, waiting for transfers between devices, step(): lax.psum_scatter(t[0], 'dp', scatter_dimension=1, tiled=True)  316 us
    all_gather x3, waiting for transfers between devices, step(): whole = [lax.all_gather(one[0], 'dp', axis=1, tiled=True) for one in new]  251 us
    unnamed x13, local copies, waits for them, and re-layouts  34.1 us
    convert_element_type x3, other arithmetic, adamw(): return ((w - 0.02 * step).astype(jnp.bfloat16), m, v)  25.1 us
  transfers between devices with their start and end apart: 6, of which 6 were waited for; matrix products, arithmetic and copies ran while one was open for 4% of the time, Pallas kernels for 0%

commit v1 on v0

v1 whole, which is shorter than its diff:
```python
import functools

import jax
import jax.numpy as jnp
from jax import lax
from jax.experimental import pallas as pl
from jax.experimental.pallas import tpu as pltpu
from jax.sharding import PartitionSpec as P

MESH = pl.DeviceIdType.MESH
F32, BF16 = jnp.float32, jnp.bfloat16
STEPS = ((0, 0), (1, 0), (0, 1), (1, 1), (2, 0), (2, 1))
ROWS = ((32, 8192), (512, 512))
COLS = 512


def adamw(w, m, v, g):
    m = 0.9 * m + 0.1 * g
    v = 0.95 * v + 0.05 * g * g
    step = m * lax.rsqrt(v + 1e-8) + 0.1 * w
    return (w - 0.02 * step).astype(jnp.bfloat16), m, v


def tiles(shape, body):
    across = shape[1] // COLS

    def one(i, _):
        if across == 1:
            r, c = i, 0
            body((pl.ds(pl.multiple_of(r * 16, 16), 16), pl.ds(0, COLS)))
        else:
            r, c = i // across, i % across
            body((pl.ds(pl.multiple_of(r * 16, 16), 16), pl.ds(pl.multiple_of(c * COLS, COLS), COLS)))
        return _

    lax.fori_loop(0, shape[0] // 16 * across, one, 0, unroll=2)


def kernel(*refs):
    it = iter(refs)

    def take(n):
        return [next(it) for _ in range(n)]

    g, w, m, v = take(3), take(3), take(3), take(3)
    w_out, g_out = take(3), take(3)
    pt, r1, r2, own, w_in, m_in, v_in = (take(2) for _ in range(7))
    d2d_s, d2d_r, l1_s, l1_r, l2_s, l2_r, ag_s, ag_r, agc_s, agc_r = take(10)
    own_sem, opt_sem, out_sem = take(3)

    me = lax.axis_index("dp")
    core = lax.rem(me, 2)
    y = lax.rem(me // 2, 2)
    x = me // 4

    def dev(bx, by, bc):
        return bx * 4 + by * 2 + bc

    partner = dev(x, y, 1 - core)
    nx, ny = dev(1 - x, y, core), dev(x, 1 - y, core)
    first, second = (nx, ny), (ny, nx)

    def chip(colour, block):
        f, s = ((1, 0), (1, 1), (0, 1), (0, 0))[block]
        fx, fy = (f, s) if colour == 0 else (s, f)
        return (1 - x if fx else x), (1 - y if fy else y)

    def kind(step):
        return 1 if STEPS[step][0] == 2 else 0

    def at(step):
        return step - 4 if kind(step) else step

    def region(ref, step, colour, device):
        n = ROWS[kind(step)][0]
        start = pl.multiple_of(device * (2 * n) + colour * n, n)
        return ref.at[STEPS[step][1], pl.ds(start, n)]

    def block_of(ref, step, colour, block, bc):
        return region(ref, step, colour, dev(*chip(colour, block), bc))

    def remote(src, dst, ss, rs, device):
        return pltpu.make_async_remote_copy(src, dst, ss, rs, device_id={"dp": device}, device_id_type=MESH)

    def load_own(step, colour, block):
        return pltpu.make_async_copy(
            block_of(g[STEPS[step][0]], step, colour, block, core), own[kind(step)].at[colour, block], own_sem.at[kind(step), colour, block]
        )

    def load_opt(step, colour):
        q, (which, layer), k = kind(step), STEPS[step], ROWS[kind(step)][0]
        here = pl.ds(colour * k, k)
        return (
            pltpu.make_async_copy(region(w[which], step, colour, me), w_in[q].at[colour], opt_sem.at[q, colour, 0]),
            pltpu.make_async_copy(m[which].at[layer, here], m_in[q].at[colour], opt_sem.at[q, colour, 1]),
            pltpu.make_async_copy(v[which].at[layer, here], v_in[q].at[colour], opt_sem.at[q, colour, 2]),
        )

    def d2d(step, colour, block):
        return remote(
            block_of(g[STEPS[step][0]], step, colour, block, 1 - core),
            pt[kind(step)].at[at(step), colour, block],
            d2d_s.at[step, colour, block],
            d2d_r.at[step, colour, block],
            partner,
        )

    def sum1(step, colour, block):
        q, i = kind(step), at(step)
        return remote(
            pt[q].at[i, colour, block], r1[q].at[i, colour, block], l1_s.at[step, colour, block], l1_r.at[step, colour, block], first[colour]
        )

    def sum2(step, colour):
        q, i = kind(step), at(step)
        return remote(r1[q].at[i, colour, 1], r2[q].at[i, colour], l2_s.at[step, colour], l2_r.at[step, colour], second[colour])

    def out_block(step, colour, block):
        return block_of(w_out[STEPS[step][0]], step, colour, block, core)

    def keep(step, colour):
        q, i, (which, layer), k = kind(step), at(step), STEPS[step], ROWS[kind(step)][0]
        return (
            pltpu.make_async_copy(r2[q].at[i, colour], out_block(step, colour, 3), out_sem.at[step, colour, 0]),
            pltpu.make_async_copy(r1[q].at[i, colour, 0], g_out[which].at[layer, pl.ds(colour * k, k)], out_sem.at[step, colour, 1]),
        )

    def gather(step, colour, hop):
        q, i = kind(step), at(step)
        src = out_block(step, colour, 2) if hop == 2 else r2[q].at[i, colour]
        dst = out_block(step, colour, 2 if hop == 2 else 3)
        return remote(src, dst, ag_s.at[step, colour, hop], ag_r.at[step, colour, hop], second[colour] if hop == 0 else first[colour])

    def across(step, colour, block):
        q, i = kind(step), at(step)
        src = r2[q].at[i, colour] if block == 3 else out_block(step, colour, block)
        return remote(src, out_block(step, colour, block), agc_s.at[step, colour, block], agc_r.at[step, colour, block], partner)

    def stage1(step):
        for block in (0, 1):
            for colour in (0, 1):
                q, i = kind(step), at(step)
                load_own(step, colour, block).wait()
                d2d(step, colour, block).wait_recv()
                a, b = own[q].at[colour, block], pt[q].at[i, colour, block]

                def add(t, a=a, b=b):
                    b[t] = (a[t].astype(F32) + b[t].astype(F32)).astype(BF16)

                tiles(ROWS[q], add)
                sum1(step, colour, block).start()
                if step + 1 < len(STEPS):
                    load_own(step + 1, colour, block).start()
        for block, later in ((0, 2), (1, 2), (2, 0), (3, 0)):
            for colour in (0, 1):
                if step + later < len(STEPS):
                    d2d(step + later, colour, block).start()

    def stage2(step):
        for colour in (0, 1):
            q, i = kind(step), at(step)
            load_own(step, colour, 2).wait()
            d2d(step, colour, 2).wait_recv()
            sum1(step, colour, 1).wait_recv()
            a, b, c = own[q].at[colour, 2], pt[q].at[i, colour, 2], r1[q].at[i, colour, 1]

            def add(t, a=a, b=b, c=c):
                c[t] = (a[t].astype(F32) + b[t].astype(F32) + c[t].astype(F32)).astype(BF16)

            tiles(ROWS[q], add)
            sum2(step, colour).start()
            if step + 1 < len(STEPS):
                load_own(step + 1, colour, 2).start()

    def stage3(step):
        for colour in (0, 1):
            q, i = kind(step), at(step)
            load_own(step, colour, 3).wait()
            for c in load_opt(step, colour):
                c.wait()
            d2d(step, colour, 3).wait_recv()
            sum1(step, colour, 0).wait_recv()
            sum2(step, colour).wait_recv()
            a, b, c, d = own[q].at[colour, 3], pt[q].at[i, colour, 3], r1[q].at[i, colour, 0], r2[q].at[i, colour]
            wr, mr, vr = w_in[q].at[colour], m_in[q].at[colour], v_in[q].at[colour]

            def update(t, a=a, b=b, c=c, d=d, wr=wr, mr=mr, vr=vr):
                grad = (a[t].astype(F32) + b[t].astype(F32) + (c[t].astype(F32) + d[t].astype(F32))).astype(BF16)
                c[t] = grad
                d[t] = adamw(wr[t].astype(F32), mr[t], vr[t], grad.astype(F32))[0]

            tiles(ROWS[q], update)
            gather(step, colour, 0).start()
            gather(step, colour, 1).start()
            across(step, colour, 3).start()
            for c in keep(step, colour):
                c.start()
            if step + 1 < len(STEPS):
                load_own(step + 1, colour, 3).start()
                for c in load_opt(step + 1, colour):
                    c.start()

    def stage4(step):
        for colour in (0, 1):
            gather(step, colour, 0).wait_recv()
            gather(step, colour, 2).start()
            across(step, colour, 2).start()

    def stage5(step):
        for hop, block in ((1, 0), (2, 1)):
            for colour in (0, 1):
                gather(step, colour, hop).wait_recv()
                across(step, colour, block).start()

    def finish():
        for step in range(len(STEPS)):
            for colour in (0, 1):
                for block in range(4):
                    d2d(step, colour, block).wait_send()
                    across(step, colour, block).wait()
                for block in (0, 1):
                    sum1(step, colour, block).wait_send()
                sum2(step, colour).wait_send()
                for hop in range(3):
                    gather(step, colour, hop).wait_send()
                for c in keep(step, colour):
                    c.wait()

    for block in range(4):
        for colour in (0, 1):
            load_own(0, colour, block).start()
    for colour in (0, 1):
        for c in load_opt(0, colour):
            c.start()
    barrier = pltpu.get_barrier_semaphore()
    for other in (partner, nx, ny):
        pl.semaphore_signal(barrier, inc=1, device_id={"dp": other}, device_id_type=MESH)
    pl.semaphore_wait(barrier, 3)
    for step in (0, 1):
        for block in (0, 1):
            for colour in (0, 1):
                d2d(step, colour, block).start()

    for stage, step in ORDER:
        (stage1, stage2, stage3, stage4, stage5)[stage - 1](step)
    finish()


ORDER = (
    (1, 0), (1, 1), (1, 2), (2, 0), (1, 3), (2, 1), (1, 4), (2, 2), (1, 5), (3, 0), (2, 3), (3, 1), (2, 4), (3, 2), (2, 5), (3, 3),
    (4, 0), (3, 4), (4, 1), (3, 5), (4, 2), (5, 0), (4, 3), (5, 1), (4, 4), (5, 2), (4, 5), (5, 3), (5, 4), (5, 5),
)


def solution(mesh):
    def step(*arrays):
        terms, weights, m, v = (arrays[i : i + 3] for i in (0, 3, 6, 9))
        terms = [t[0] for t in terms]
        any_, dma = pl.BlockSpec(memory_space=pl.ANY), pltpu.SemaphoreType.DMA
        n = len(STEPS)

        def bufs(dtype, *lead):
            return [pltpu.VMEM((*(k[q] if isinstance(k, tuple) else k for k in lead), *ROWS[q]), dtype) for q in (0, 1)]

        slots = (4, 2)
        outs = pl.pallas_call(
            kernel,
            out_shape=[jax.ShapeDtypeStruct(w.shape, BF16) for w in weights] + [jax.ShapeDtypeStruct(one.shape, BF16) for one in m],
            in_specs=[any_] * 12,
            out_specs=[any_] * 6,
            scratch_shapes=[
                *bufs(BF16, slots, 2, 4),
                *bufs(BF16, slots, 2, 2),
                *bufs(BF16, slots, 2),
                *bufs(BF16, 2, 4),
                *bufs(BF16, 2),
                *bufs(F32, 2),
                *bufs(F32, 2),
                dma((n, 2, 4)), dma((n, 2, 4)),
                dma((n, 2, 2)), dma((n, 2, 2)),
                dma((n, 2)), dma((n, 2)),
                dma((n, 2, 3)), dma((n, 2, 3)),
                dma((n, 2, 4)), dma((n, 2, 4)),
                dma((2, 2, 4)), dma((2, 2, 3)), dma((n, 2, 2)),
            ],
            compiler_params=pltpu.CompilerParams(collective_id=0, has_side_effects=True, vmem_limit_bytes=67043328),
        )(*terms, *weights, *m, *v)
        whole, grads = outs[:3], [one.astype(F32) for one in outs[3:]]
        new_m = [0.9 * one + 0.1 * grad for one, grad in zip(m, grads, strict=True)]
        new_v = [0.95 * one + 0.05 * grad * grad for one, grad in zip(v, grads, strict=True)]
        return (*whole, *new_m, *new_v)

    all_of, cut = P(None, None, None), P(None, "dp", None)
    return jax.shard_map(
        step,
        mesh=mesh,
        in_specs=(P(("rep", "dp"), None, None, None),) * 3 + (all_of,) * 3 + (cut,) * 6,
        out_specs=(P("rep", None, None),) * 3 + (P("rep", "dp", None),) * 6,
        check_vma=False,
    )
```

time: 642 us -> 473 us (0.74)
  waiting for transfers between devices: 569 us -> 0 us
  Pallas kernels: 0 us -> 418 us
  between operations: 14.1 us -> 0.73 us
    pallas_call x0 -> x1, Pallas kernels: none -> 418 us  [step(): pl.pallas_call(kernel, out_shape=[jax.ShapeDtypeStruct(w.shape, BF16) for...]
    reduce_scatter x3 -> x0, waiting for transfers between devices: 316 us -> none  [step(): lax.psum_scatter(t[0], 'dp', scatter_dimension=1, tiled=True)]
    all_gather x3 -> x0, waiting for transfers between devices: 251 us -> none  [step(): whole = [lax.all_gather(one[0], 'dp', axis=1, tiled=True) for one in new]]
    convert_element_type x3 -> x0, other arithmetic: 25.1 us -> none  [adamw(): return ((w - 0.02 * step).astype(jnp.bfloat16), m, v)]
    add x0 -> x2, other arithmetic: none -> 20 us  [step(): 0.95 * one + 0.05 * grad * grad]
    unnamed x13 -> x25, local copies, waits for them, and re-layouts: 34.1 us -> 33.7 us
  transfers between devices with their start and end apart: 6 -> 0, of which waited for: 6 -> 0; matrix products, arithmetic and copies ran while one was open for 4% -> 0% of each run, Pallas kernels for 0% -> 0%
where the time goes in v1:
time: 473 us
  Pallas kernels  418 us (88%)
  local copies, waits for them, and re-layouts  33.7 us (7%)
  other arithmetic  20 us (4%)
    pallas_call x1, Pallas kernels, step(): pl.pallas_call(kernel, out_shape=[jax.ShapeDtypeStruct(w.shape, BF16) for...  418 us
    unnamed x25, local copies, waits for them, and re-layouts  33.7 us
    add x2, other arithmetic, step(): 0.95 * one + 0.05 * grad * grad  20 us

profile of v1, /device:TPU:0, one launch (start us, length us, event | category | flops | bytes accessed | tf_op | source)
XLA Modules:
  0.0 472.5 jit_solution(6266836012051729393)
XLA Ops:
  0.6 418.1 %shard_map.187 = (bf16[2,512,8192]{2,1,0:T(8,128)(2,1)}, bf16[2,512,8192]{2,1,0:T(8,128)(2,1)}, bf16[2,8192,512]{2,1,0:T(8,128)(2,1)}, bf16[2,64,8192]{2,1,0:T(8...) custom-call(bf16[2,512,8192]{2,1,0:T(8,128)(2,1)} %bitcast.3, bf16[2,512,8192]{2,1,0:T(8,128)(2,1)} %bitcast.4, ...), custom_call_target="tpu_custom_call" | custom-call | tf_op jit(solution)/shard_map/pallas_call | solution.py:266
  418.7 0.0 copy-start
  418.7 0.0 copy-start.1
  418.7 0.0 copy-start.2
  418.8 14.7 %fusion.3 = (f32[2,64,8192]{2,1,0:T(8,128)}, f32[2,64,8192]{2,1,0:T(8,128)}, f32[2,64,8192]{2,1,0:T(8,128)}, f32[2,64,8192]{2,1,0:T(8,128)}) fusion(bf16[2,64,8192]{2,1,0:T(8,128)(2,1)} %get-tuple-element.18, f32[2,64,8192]{2,1,0:T(8,128)} %refs_9_.1, f32[2,64,8192]{2,1,0:T(8,128)} %refs_6_.1, bf16[2,64,8192]{2,1,0:T(8,128)(2,1)} %get-tuple-element.19, ...), kind=kLoop, calls=%fused_computation.9 | loop fusion | flops 16777216 | bytes 37748736 | tf_op jit(solution)/shard_map/add | solution.py:290
  433.4 0.0 copy-done
  433.4 0.0 copy-done.1
  433.4 1.2 copy-done.2
  434.7 0.0 slice-start.4
  434.7 0.0 slice-start.5
  434.7 5.3 %fusion.5 = (f32[2,1024,512]{2,1,0:T(8,128)}, f32[2,1024,512]{2,1,0:T(8,128)}) fusion(bf16[2,1024,512]{2,1,0:T(8,128)(2,1)S(1)} %copy-done.2, f32[2,1024,512]{2,1,0:T(8,128)S(1)} %copy-done.1, f32[2,1024,512]{2,1,0:T(8,128)S(1)} %copy-done), kind=kLoop, calls=%fused_computation.11 | loop fusion | flops 8388608 | bytes 18874368 | tf_op jit(solution)/shard_map/add | solution.py:290
  440.0 16.8 %copy.24 = bf16[2,512,8192]{2,1,0:T(8,128)(2,1)} copy(bf16[2,512,8192]{2,1,0:T(8,128)(2,1)} %get-tuple-element.38) | data formatting | bytes 33554432
  456.8 0.0 slice-done.4
  456.8 0.0 slice-done.5
  456.8 0.0 slice-done.6
  456.8 0.0 slice-done.7
  456.9 0.0 slice-start.2
  456.9 0.0 slice-start.3
  456.9 8.5 %copy.25 = bf16[2,512,8192]{2,1,0:T(8,128)(2,1)} copy(bf16[2,512,8192]{2,1,0:T(8,128)(2,1)S(1)} %bitcast.9) | data formatting | bytes 33554432
  465.4 0.0 slice-done
  465.4 0.0 slice-done.1
  465.4 0.0 slice-done.2
  465.4 1.0 slice-done.3
  466.4 6.2 %copy.26 = bf16[2,8192,512]{2,1,0:T(8,128)(2,1)} copy(bf16[2,8192,512]{2,1,0:T(8,128)(2,1)S(1)} %bitcast.7) | data formatting | bytes 33554432
  (6 shorter events, 0.0 us)
Async XLA Ops:
  418.7 14.7 %copy-start = (f32[2,1024,512]{2,1,0:T(8,128)S(1)}, f32[2,1024,512]{2,1,0:T(8,128)}, u32[]{:S(2)}) copy-start(f32[2,1024,512]{2,1,0:T(8,128)} %refs_8_.1) | copy-start | bytes 12582916
  418.7 14.7 %copy-start.1 = (f32[2,1024,512]{2,1,0:T(8,128)S(1)}, f32[2,1024,512]{2,1,0:T(8,128)}, u32[]{:S(2)}) copy-start(f32[2,1024,512]{2,1,0:T(8,128)} %refs_11_.1) | copy-start | bytes 12582916
  418.7 15.9 %copy-start.2 = (bf16[2,1024,512]{2,1,0:T(8,128)(2,1)S(1)}, bf16[2,1024,512]{2,1,0:T(8,128)(2,1)}, u32[]{:S(2)}) copy-start(bf16[2,1024,512]{2,1,0:T(8,128)(2,1)} %get-tuple-element.20) | copy-start | bytes 6291460
  434.7 22.2 %slice-start.4 = ((s8[16777216]{0:T(1024)(128)(4,1)}), s8[4194304]{0:T(1024)(128)(4,1)S(1)}, s32[]{:S(2)}) async-start(s8[16777216]{0:T(1024)(128)(4,1)} %bitcast.8), calls=%async_computation.4 | async-start | bytes 8388608
  434.7 22.2 %slice-start.5 = ((s8[16777216]{0:T(1024)(128)(4,1)}), s8[4194304]{0:T(1024)(128)(4,1)S(1)}, s32[]{:S(2)}) async-start(s8[16777216]{0:T(1024)(128)(4,1)} %bitcast.8), calls=%async_computation.5 | async-start | bytes 8388608
  440.0 16.8 %slice-start.6 = ((s8[16777216]{0:T(1024)(128)(4,1)}), s8[4194304]{0:T(1024)(128)(4,1)S(1)}, s32[]{:S(2)}) async-start(s8[16777216]{0:T(1024)(128)(4,1)} %bitcast.8), calls=%async_computation.6 | async-start | bytes 8388608
  440.0 16.9 %slice-start.7 = ((s8[16777216]{0:T(1024)(128)(4,1)}), s8[4194304]{0:T(1024)(128)(4,1)S(1)}, s32[]{:S(2)}) async-start(s8[16777216]{0:T(1024)(128)(4,1)} %bitcast.8), calls=%async_computation.7 | async-start | bytes 8388608
  440.0 25.4 %slice-start = ((s8[16777216]{0:T(1024)(128)(4,1)}), s8[4194304]{0:T(1024)(128)(4,1)S(1)}, s32[]{:S(2)}) async-start(s8[16777216]{0:T(1024)(128)(4,1)} %bitcast.6), calls=%async_computation | async-start | bytes 8388608
  440.0 25.4 %slice-start.1 = ((s8[16777216]{0:T(1024)(128)(4,1)}), s8[4194304]{0:T(1024)(128)(4,1)S(1)}, s32[]{:S(2)}) async-start(s8[16777216]{0:T(1024)(128)(4,1)} %bitcast.6), calls=%async_computation.1 | async-start | bytes 8388608
  456.9 8.5 %slice-start.2 = ((s8[16777216]{0:T(1024)(128)(4,1)}), s8[4194304]{0:T(1024)(128)(4,1)S(1)}, s32[]{:S(2)}) async-start(s8[16777216]{0:T(1024)(128)(4,1)} %bitcast.6), calls=%async_computation.2 | async-start | bytes 8388608
  456.9 9.5 %slice-start.3 = ((s8[16777216]{0:T(1024)(128)(4,1)}), s8[4194304]{0:T(1024)(128)(4,1)S(1)}, s32[]{:S(2)}) async-start(s8[16777216]{0:T(1024)(128)(4,1)} %bitcast.6), calls=%async_computation.3 | async-start | bytes 8388608
